TPU v7x, 32 devices: a whole 2x2x4 slice. The times are simulated.
32 devices in a mesh: outer: 4 (over y, x), inner: 8 (over z, core).
Axes of the slice: x: 2, y: 2, z: 4, core: 2. Of those that a mesh axis runs over, the one named last changes fastest.
Arguments:
- acts: bfloat16 [32, 2, 512, 512], P(('outer', 'inner')), may hold values from -6 to 6
- cotangent: bfloat16 [32, 2, 512, 512], P(('outer', 'inner')), may hold values from -6 to 6
- residual: float32 [32, 2048, 128], P(('outer', 'inner')), may hold values from -0.6 to 0.6
- owner_residual: float32 [32, 256, 128], P(('outer', 'inner')), may hold values from -3 to 3
- in_count: int32 [32, 2, 8], P(('outer', 'inner')), may hold values from 1 to 128, as said below
- in_rank: int32 [32, 2, 2048], P(('outer', 'inner')), may hold values from 0 to 255, as said below
- out_count: int32 [32, 2], P(('outer', 'inner')), may hold values from 1 to 128
- out_rank: int32 [32, 2, 256], P(('outer', 'inner')), may hold values from 0 to 255, as said below
Outputs:
- applied: bfloat16 [512, 512], replicated
- new_residual: float32 [32, 2048, 128], P(('outer', 'inner'))
- new_owner_residual: float32 [32, 256, 128], P(('outer', 'inner'))
Inputs may be any that keep to these rules, and one draw needn't show every extreme that they name: `in_count`: each step has one owner that receives 128 blocks from every replica. `in_rank`: for each replica, step and owner, the ranks of that owner's 256 blocks are a permutation of 0 to 255. `out_rank`: for each replica and step a permutation of 0 to 255.
All inputs are finite; a program needn't handle non-finite values.
Results may differ from a plain program's by a relative error of at most 0.0065.
Values may be sent and summed in bfloat16 or wider, within the bound.
A program may use at most 64 MiB of HBM per device.

v0:
```python
import functools
import math

import jax
import jax.numpy as jnp
from jax import lax
from jax.experimental import pallas as pl
from jax.experimental.pallas import tpu as pltpu
from jax.sharding import PartitionSpec as P

step_size = 0.0625


def select_blocks(resid, grad, ranks_flat, counts, owners, region, width):
    blocks = resid.shape[0]
    accum = (resid + grad.reshape(blocks, width)).reshape(owners, region, width)
    ranks = ranks_flat.reshape(owners, region)
    chosen = (ranks < counts[:, None])[..., None]
    new_resid = jnp.where(chosen, jnp.float32(0.0), accum).reshape(blocks, width)
    return (accum, ranks, chosen, new_resid)


def pack_slots(accum, ranks, counts, slots, region):
    order = lax.iota(jnp.int32, slots)
    picks = (ranks[:, None, :] == order[None, :, None]) & (
        order[None, :, None] < counts[:, None, None]
    )
    picks_f = picks.astype(jnp.float32)
    places = lax.iota(jnp.int32, region).astype(jnp.float32)
    packed = jnp.einsum("nkr,nrd->nkd", picks_f, accum, precision=lax.Precision.HIGHEST)
    where_at = jnp.einsum("nkr,r->nk", picks_f, places, precision=lax.Precision.HIGHEST)
    return (packed, where_at)


def unpack_slots(arrived, spots, region, width):
    places = lax.iota(jnp.int32, region).astype(jnp.float32)
    placed = (spots.reshape(-1)[:, None] == places[None, :]).astype(jnp.float32)
    return jnp.einsum(
        "mr,md->rd", placed, arrived.reshape(-1, width), precision=lax.Precision.HIGHEST
    )


def owner_section(pod_sum, oresid, ranks_out, count_out):
    owner_acc = pod_sum + oresid
    passed = (ranks_out < count_out)[:, None]
    outgoing = jnp.where(passed, owner_acc, jnp.float32(0.0))
    kept = jnp.where(passed, jnp.float32(0.0), owner_acc)
    return (outgoing, kept)


def per_device(acts, cotangent, residual, owner_residual, in_count, in_rank, out_count, out_rank):
    owners = lax.axis_size("inner")
    steps = acts.shape[1]
    tokens = acts.shape[2]
    rows = acts.shape[3]
    cols = cotangent.shape[3]
    blocks = residual.shape[1]
    width = residual.shape[2]
    region = blocks // owners
    slots = max(1, region // 2)
    scale = 1.0 / math.sqrt(tokens * owners)
    resid = residual[0]
    oresid = owner_residual[0]
    crosses = []
    packs = []
    spots_all = []
    for step in range(steps):
        grad = (
            jnp.einsum(
                "tr,tc->rc", acts[0, step], cotangent[0, step], preferred_element_type=jnp.float32
            )
            * scale
        )
        counts = in_count[0, step]
        accum, ranks, chosen, resid = select_blocks(
            resid, grad, in_rank[0, step], counts, owners, region, width
        )
        packed, where_at = pack_slots(accum, ranks, counts, slots, region)
        packs.append(packed)
        spots_all.append(where_at)
    arrived, spots = (
        lax.all_to_all(
            jnp.concatenate(packs, axis=1), "inner", split_axis=0, concat_axis=0, tiled=True
        ),
        lax.all_to_all(
            jnp.concatenate(spots_all, axis=1), "inner", split_axis=0, concat_axis=0, tiled=True
        ),
    )
    outgoings = []
    for step in range(steps):
        pod_sum = unpack_slots(
            arrived[:, step * slots : (step + 1) * slots],
            spots[:, step * slots : (step + 1) * slots],
            region,
            width,
        )
        outgoing, oresid = owner_section(pod_sum, oresid, out_rank[0, step], out_count[0, step])
        outgoings.append(outgoing)
    summed = lax.psum(jnp.stack(outgoings), "outer")
    for step in range(steps):
        crosses.append(summed[step])
    deltas = []
    for cross in crosses:
        delta = cross.astype(jnp.bfloat16)
        deltas.append(lax.all_gather(delta, "inner", axis=0, tiled=True))
    total = deltas[0].astype(jnp.float32)
    for later in deltas[1:]:
        total = total + later.astype(jnp.float32)
    applied = (-step_size * total).astype(jnp.bfloat16)
    return (applied.reshape(rows, cols), resid[None], oresid[None])


LANES = 128
F32 = jnp.float32
BF16 = jnp.bfloat16


def fused_kernel(
    dims,
    acts_hbm, cot_hbm, res_hbm, ores_hbm, cnt_hbm, rank_hbm, ocnt_hbm, orank_hbm,
    applied_ref, resid_ref, nores_ref,
    ores_ref, cnt_ref, rank_ref, ocnt_ref, orank_ref, small_sem,
    acts_v, cot_v, res_v, rk_ref, rp_ref, mt_ref, rsend, rrecv, rall_ref, oh_ref,
    send, recv, xsend, xrecv, ag,
    in_sem, rs_sem, rr_sem, s_sem, r_sem, xs_sem, xr_sem,
    zs_sem, zr_sem, os_sem, or_sem, ps_sem, pr_sem,
):
    n_in, n_out, steps, scale, region, slots, width = dims
    rows, cols = acts_v.shape[2], cot_v.shape[2]
    cpr = cols // width
    rpr = region // cpr
    halves = region // LANES
    rpc = LANES // rpr
    n_z = n_in // 2
    big = float(region)
    me = lax.axis_index("inner")
    pod = lax.axis_index("outer")
    core = lax.rem(me, 2)
    z = lax.div(me, 2)
    partner = me + 1 - 2 * core

    def inner(d):
        return lax.rem(me + d, n_in)

    def outer(d):
        return lax.rem(pod + d, n_out)

    def remote(src, dst, ssem, rsem, **device):
        return pltpu.make_async_remote_copy(
            src_ref=src, dst_ref=dst, send_sem=ssem, recv_sem=rsem,
            device_id=device, device_id_type=pl.DeviceIdType.MESH,
        )

    small = [
        pltpu.make_async_copy(src, dst, small_sem.at[k])
        for k, (src, dst) in enumerate(
            ((rank_hbm, rank_ref), (cnt_hbm, cnt_ref), (orank_hbm, orank_ref), (ocnt_hbm, ocnt_ref), (ores_hbm, ores_ref))
        )
    ]
    for copy in small:
        copy.start()
    loads = []
    for s in range(steps):
        pair = [
            pltpu.make_async_copy(acts_hbm.at[s], acts_v.at[s], in_sem.at[2 * s]),
            pltpu.make_async_copy(cot_hbm.at[s], cot_v.at[s], in_sem.at[2 * s + 1]),
        ]
        for copy in pair:
            copy.start()
        loads.append(pair)
        if s == 0:
            res_load = pltpu.make_async_copy(res_hbm, res_v, in_sem.at[2 * steps])
            res_load.start()

    barrier = pltpu.get_barrier_semaphore()
    for d in range(1, n_in):
        pl.semaphore_signal(barrier, inc=1, device_id={"inner": inner(d)}, device_id_type=pl.DeviceIdType.MESH)
    for d in range(1, n_out):
        pl.semaphore_signal(barrier, inc=1, device_id={"outer": outer(d)}, device_id_type=pl.DeviceIdType.MESH)

    rk_ref[...] = jnp.full(rk_ref.shape, big, F32)
    for copy in small:
        copy.wait()
    for s in range(steps):
        for j in range(n_in):
            row = rank_ref[s : s + 1, j * region : (j + 1) * region]
            rk_ref[s * n_in + j : s * n_in + j + 1, :] = jnp.where(
                row < cnt_ref[s : s + 1, j : j + 1], row.astype(F32), big
            )
        row = orank_ref[s : s + 1, :]
        rk_ref[steps * n_in + s : steps * n_in + s + 1, :] = jnp.where(
            row < ocnt_ref[0:1, s : s + 1], row.astype(F32), big
        )
    old = lax.broadcasted_iota(jnp.int32, (region, region), 0)
    new = lax.broadcasted_iota(jnp.int32, (region, region), 1)
    shift = rpr.bit_length() - 1
    perm = jnp.where(old == (new & (rpr - 1)) * cpr + (new >> shift), 1.0, 0.0).astype(BF16)
    rp = jnp.dot(rk_ref[...].astype(BF16), perm, preferred_element_type=F32)
    rp_ref[...] = rp
    n_rk = rk_ref.shape[0]

    def eye(n):
        return jnp.where(
            lax.broadcasted_iota(jnp.int32, (n, LANES), 0) == lax.broadcasted_iota(jnp.int32, (n, LANES), 1), 1.0, 0.0
        ).astype(BF16)

    def turned(values):
        return lax.dot_general(
            values.astype(BF16), eye(values.shape[0]), (((0,), (0,)), ((), ())), preferred_element_type=F32
        ).astype(BF16)

    def spread(table, index, n):
        pick = jnp.where(lax.broadcasted_iota(jnp.int32, (LANES, n), 0) == index, 1.0, 0.0).astype(BF16)
        return jnp.dot(table, pick, preferred_element_type=F32)

    mt_ref[...] = turned(jnp.where(rp < big, 1.0, 0.0))
    for j in range(n_in):
        for s in range(steps):
            for h in range(halves):
                rsend[j, s * halves + h : s * halves + h + 1, :] = rp_ref[
                    s * n_in + j : s * n_in + j + 1, h * LANES : (h + 1) * LANES
                ]
    pl.semaphore_wait(barrier, n_in - 1 + n_out - 1)
    sends = []
    for d in range(1, n_in):
        copy = remote(rsend.at[inner(d)], rrecv.at[me], rs_sem.at[d], rr_sem.at[me], inner=inner(d))
        copy.start()
        sends.append(copy)

    order = []
    chunks = rows // LANES
    for a in range((chunks + 1) // 2):
        order.append(a)
        if chunks - 1 - a != a:
            order.append(chunks - 1 - a)

    def packet(s, j):
        return remote(send.at[s, j], recv.at[s, pl.ds(pl.multiple_of(me * slots, slots), slots)],
                      s_sem.at[s, j], r_sem.at[s, me], inner=j)

    slot_id = lax.broadcasted_iota(jnp.int32, (slots, region), 0).astype(F32)
    for s in range(steps):
        for copy in loads[s]:
            copy.wait()
        if s == 0:
            res_load.wait()
        for q in order:
            g = lax.dot_general(
                acts_v[s, :, q * LANES : (q + 1) * LANES], cot_v[s], (((0,), (0,)), ((), ())),
                preferred_element_type=F32,
            ) * scale
            for half in range(rpc):
                j = q * rpc + half
                chosen = spread(mt_ref[...], s * n_in + j, width)
                picks = jnp.where(rp_ref[s * n_in + j : s * n_in + j + 1, :] == slot_id, 1.0, 0.0).astype(BF16)
                parts = []
                for c in range(cpr):
                    where_at = pl.ds(region * j + c, rpr, stride=cpr)
                    acc = res_v[where_at, :] + g[half * rpr : (half + 1) * rpr, c * width : (c + 1) * width]
                    kept = jnp.where(chosen[c * rpr : (c + 1) * rpr] > 0.5, 0.0, acc)
                    (resid_ref if s == steps - 1 else res_v)[where_at, :] = kept
                    parts.append(acc)
                packed = jnp.dot(picks, jnp.concatenate(parts, axis=0).astype(BF16), preferred_element_type=F32)
                send[s, j] = packed.astype(BF16)

                @pl.when(me != j)
                def _():
                    packet(s, j).start()


    rrecv[me] = rsend[me]
    for d in range(1, n_in):
        i = inner(d)
        remote(rrecv.at[i], rrecv.at[i], rs_sem.at[d], rr_sem.at[i], inner=i).wait_recv()
    for i in range(n_in):
        for s in range(steps):
            for h in range(halves):
                rall_ref[s * n_in + i : s * n_in + i + 1, h * LANES : (h + 1) * LANES] = rrecv[
                    i, s * halves + h : s * halves + h + 1, :
                ]
    rt = turned(rall_ref[...])
    lane_id = lax.broadcasted_iota(jnp.int32, (region, slots), 1).astype(F32)
    for s in range(steps):
        for i in range(n_in):
            oh_ref[s, :, i * slots : (i + 1) * slots] = jnp.where(
                spread(rt, s * n_in + i, slots) == lane_id, 1.0, 0.0
            ).astype(BF16)

    oresid = jnp.concatenate([ores_ref[pl.ds(c, rpr, stride=cpr), :] for c in range(cpr)], axis=0)
    for s in range(steps):
        recv[s, pl.ds(pl.multiple_of(me * slots, slots), slots)] = send[s, me]
        for d in range(1, n_in):
            i = inner(d)
            spot = recv.at[s, pl.ds(pl.multiple_of(i * slots, slots), slots)]
            remote(spot, spot, s_sem.at[s, 0], r_sem.at[s, i], inner=i).wait_recv()
        oacc = jnp.dot(oh_ref[s], recv[s], preferred_element_type=F32) + oresid
        passed = spread(mt_ref[...], steps * n_in + s, width) > 0.5
        outgoing = jnp.where(passed, oacc, 0.0).astype(BF16)
        oresid = jnp.where(passed, 0.0, oacc)
        for c in range(n_out):
            xsend[s, c] = outgoing[c * rpr : (c + 1) * rpr]
        for d in range(1, n_out):
            copy = remote(xsend.at[s, outer(d)], xrecv.at[s, pod], xs_sem.at[s, d], xr_sem.at[s, pod], outer=outer(d))
            copy.start()
            sends.append(copy)
    for c in range(cpr):
        nores_ref[pl.ds(c, rpr, stride=cpr), :] = oresid[c * rpr : (c + 1) * rpr]

    total = jnp.zeros((rpr, width), F32)
    for s in range(steps):
        cross = xsend[s, pod].astype(F32)
        for d in range(1, n_out):
            i = outer(d)
            remote(xrecv.at[s, i], xrecv.at[s, i], xs_sem.at[s, d], xr_sem.at[s, i], outer=i).wait_recv()
            cross = cross + xrecv[s, i].astype(F32)
        total = total + cross.astype(BF16).astype(F32)
    ag[core, pod, z] = (-step_size * total).astype(BF16)

    def forward(zz, slot):
        piece = ag.at[core, pod, zz]
        for d in range(1, n_out):
            copy = remote(piece, piece, os_sem.at[slot, d], or_sem.at[pod, zz], outer=outer(d))
            copy.start()
            sends.append(copy)

    def hand_over(q, slot):
        piece = ag.at[core, q]
        copy = remote(piece, piece, ps_sem.at[slot], pr_sem.at[q], inner=partner)
        copy.start()
        sends.append(copy)

    own = ag.at[core, pod, z]
    for d in range(1, n_z):
        copy = remote(own, own, zs_sem.at[d], zr_sem.at[z], inner=inner(2 * d))
        copy.start()
        sends.append(copy)
    forward(z, 0)
    for d in range(1, n_z):
        zz = lax.rem(z + d, n_z)
        piece = ag.at[core, pod, zz]
        remote(piece, piece, zs_sem.at[d], zr_sem.at[zz], inner=inner(2 * d)).wait_recv()
        forward(zz, d)
    hand_over(pod, 0)
    for d in range(1, n_out):
        q = outer(d)
        for zz in range(n_z):
            piece = ag.at[core, q, zz]
            remote(piece, piece, os_sem.at[0, d], or_sem.at[q, zz], outer=q).wait_recv()
        hand_over(q, d)
    for d in range(n_out):
        q = outer(d)
        piece = ag.at[1 - core, q]
        remote(piece, piece, ps_sem.at[d], pr_sem.at[q], inner=partner).wait_recv()
    for zz in range(n_z):
        for k in range(2):
            j = zz * 2 + k
            for q in range(n_out):
                applied_ref[j * rpr : (j + 1) * rpr, q * width : (q + 1) * width] = ag[k, q, zz]

    for copy in sends:
        copy.wait_send()
    for s in range(steps):
        for j in range(n_in):

            @pl.when(me != j)
            def _():
                packet(s, j).wait_send()


def hand_out(*arrays):
    n = len(arrays)

    def kernel(*refs):
        sems = refs[2 * n]
        copies = [pltpu.make_async_copy(refs[k], refs[n + k], sems.at[k]) for k in range(n)]
        for copy in copies:
            copy.start()
        for copy in copies:
            copy.wait()

    return pl.pallas_call(
        kernel,
        out_shape=tuple(jax.ShapeDtypeStruct(a.shape, a.dtype) for a in arrays),
        in_specs=[pl.BlockSpec(memory_space=pltpu.VMEM)] * n,
        out_specs=tuple([pl.BlockSpec(memory_space=pltpu.HBM)] * n),
        scratch_shapes=[pltpu.SemaphoreType.DMA((n,))],
        compiler_params=pltpu.CompilerParams(vmem_limit_bytes=4 << 20),
    )(*arrays)


def fits(owners, pods, steps, rows, cols, blocks, width, region, slots):
    if width != LANES or slots % LANES or region % LANES or region > 256 or cols % width:
        return False
    cpr = cols // width
    rpr = region // cpr
    return (
        cpr == pods and cpr * rpr == region and rpr % 16 == 0 and LANES % rpr == 0 and rpr & (rpr - 1) == 0
        and rows % LANES == 0 and owners >= 4 and owners % 2 == 0
        and rpr * owners == rows and steps * (owners + 1) <= LANES and steps * (region // LANES) <= 8
    )


def per_device_fused(acts, cotangent, residual, owner_residual, in_count, in_rank, out_count, out_rank):
    n_in = lax.axis_size("inner")
    n_out = lax.axis_size("outer")
    steps, tokens, rows = acts.shape[1:]
    cols = cotangent.shape[3]
    blocks, width = residual.shape[1:]
    region = blocks // n_in
    slots = max(1, region // 2)
    if not fits(n_in, n_out, steps, rows, cols, blocks, width, region, slots):
        return per_device(acts, cotangent, residual, owner_residual, in_count, in_rank, out_count, out_rank)
    scale = 1.0 / math.sqrt(tokens * n_in)
    rpr = region // n_out
    n_z = n_in // 2
    n_rk = -(-steps * (n_in + 1) // 16) * 16
    n_ra = -(-steps * n_in // 16) * 16
    vmem = pl.BlockSpec(memory_space=pltpu.VMEM)
    anywhere = pl.BlockSpec(memory_space=pltpu.HBM)
    dma = pltpu.SemaphoreType.DMA
    applied, resid, oresid = pl.pallas_call(
        functools.partial(fused_kernel, (n_in, n_out, steps, scale, region, slots, width)),
        out_shape=(
            jax.ShapeDtypeStruct((rows, cols), BF16),
            jax.ShapeDtypeStruct((blocks, width), F32),
            jax.ShapeDtypeStruct((region, width), F32),
        ),
        in_specs=[anywhere] * 8,
        out_specs=(vmem, vmem, vmem),
        scratch_shapes=[
            pltpu.VMEM((region, width), F32),
            pltpu.VMEM((steps, n_in), jnp.int32),
            pltpu.VMEM((steps, blocks), jnp.int32),
            pltpu.VMEM((1, steps), jnp.int32),
            pltpu.VMEM((steps, region), jnp.int32),
            dma((5,)),
            pltpu.VMEM((steps, tokens, rows), BF16),
            pltpu.VMEM((steps, tokens, cols), BF16),
            pltpu.VMEM((blocks, width), F32),
            pltpu.VMEM((n_rk, region), F32),
            pltpu.VMEM((n_rk, region), F32),
            pltpu.VMEM((region, LANES), BF16),
            pltpu.VMEM((n_in, 8, LANES), F32),
            pltpu.VMEM((n_in, 8, LANES), F32),
            pltpu.VMEM((n_ra, region), F32),
            pltpu.VMEM((steps, region, n_in * slots), BF16),
            pltpu.VMEM((steps, n_in, slots, width), BF16),
            pltpu.VMEM((steps, n_in * slots, width), BF16),
            pltpu.VMEM((steps, n_out, rpr, width), BF16),
            pltpu.VMEM((steps, n_out, rpr, width), BF16),
            pltpu.VMEM((2, n_out, n_z, rpr, width), BF16),
            dma((2 * steps + 1,)),
            dma((n_in,)),
            dma((n_in,)),
            dma((steps, n_in)),
            dma((steps, n_in)),
            dma((steps, n_out)),
            dma((steps, n_out)),
            dma((n_z,)),
            dma((n_z,)),
            dma((n_z, n_out)),
            dma((n_out, n_z)),
            dma((n_out,)),
            dma((n_out,)),
        ],
        compiler_params=pltpu.CompilerParams(collective_id=0, has_side_effects=True, vmem_limit_bytes=48 << 20),
    )(*(
        pltpu.with_memory_space_constraint(a, pltpu.HBM)
        for a in (
            acts[0], cotangent[0], residual[0], owner_residual[0], in_count[0], in_rank[0], out_count, out_rank[0]
        )
    ))
    applied, resid, oresid = hand_out(applied, resid, oresid)
    return applied, resid[None], oresid[None]


def solution(mesh):
    return jax.shard_map(
        per_device_fused,
        mesh=mesh,
        in_specs=(
            P(("outer", "inner"), None, None, None),
            P(("outer", "inner"), None, None, None),
            P(("outer", "inner"), None, None),
            P(("outer", "inner"), None, None),
            P(("outer", "inner"), None, None),
            P(("outer", "inner"), None, None),
            P(("outer", "inner"), None),
            P(("outer", "inner"), None, None),
        ),
        out_specs=(P(), P(("outer", "inner"), None, None), P(("outer", "inner"), None, None)),
        check_vma=False,
    )
```

profile of v0, /device:TPU:0, one launch (start us, length us, event | category | flops | bytes accessed | tf_op | source)
XLA Modules:
  0.0 33.6 jit_solution(12429981556202038092)
XLA Ops:
  0.6 31.8 %shard_map.103 = (bf16[512,512]{1,0:T(8,128)(2,1)S(1)}, f32[2048,128]{1,0:T(8,128)S(1)}, f32[256,128]{1,0:T(8,128)S(1)}) custom-call(bf16[2,512,512]{2,1,0:T(8,128)(2,1)} %bitcast.9, bf16[2,512,512]{2,1,0:T(8,128)(2,1)} %bitcast.10, f32[2048,128]{1,0:T(8,128)} %bitcast.11, f32[256,128]{1,0:T(8,128)} %bitcast.12, s32[2,8]{1,0:T(2,128)} %bitcast.15, ...), custom_call_target="tpu_custom_call" | custom-call | tf_op jit(solution)/shard_map/pallas_call | solution.py:421
  32.4 1.2 %shard_map.104 = (bf16[512,512]{1,0:T(8,128)(2,1)}, f32[2048,128]{1,0:T(8,128)}, f32[256,128]{1,0:T(8,128)}) custom-call(bf16[512,512]{1,0:T(8,128)(2,1)S(1)} %get-tuple-element.9.refs_0_, f32[2048,128]{1,0:T(8,128)S(1)} %get-tuple-element.10.refs_1_, f32[256,128]{1,0:T(8,128)S(1)} %get-tuple-element.11.refs_2_), custom_call_target="tpu_custom_call" | custom-call | tf_op jit(solution)/shard_map/pallas_call | solution.py:381
where the time goes:
time: 33.9 us; the launch traced here: 33.6 us
  Pallas kernels  33 us (97%)
  between operations  0.64 us (2%)
    pallas_call x1, Pallas kernels, per_device_fused(): pl.pallas_call(functools.partial(fused_kernel, (n_in, n_out, steps, scale...  31.8 us
    pallas_call x1, Pallas kernels, hand_out(): pl.pallas_call(kernel, out_shape=tuple((jax.ShapeDtypeStruct(a.shape, a.d...  1.2 us

commit v1 on v0

v1 whole, which is shorter than its diff:
```python
import functools
import math

import jax
import jax.numpy as jnp
from jax import lax
from jax.experimental import pallas as pl
from jax.experimental.pallas import tpu as pltpu
from jax.sharding import PartitionSpec as P

step_size = 0.0625


def select_blocks(resid, grad, ranks_flat, counts, owners, region, width):
    blocks = resid.shape[0]
    accum = (resid + grad.reshape(blocks, width)).reshape(owners, region, width)
    ranks = ranks_flat.reshape(owners, region)
    chosen = (ranks < counts[:, None])[..., None]
    new_resid = jnp.where(chosen, jnp.float32(0.0), accum).reshape(blocks, width)
    return (accum, ranks, chosen, new_resid)


def pack_slots(accum, ranks, counts, slots, region):
    order = lax.iota(jnp.int32, slots)
    picks = (ranks[:, None, :] == order[None, :, None]) & (
        order[None, :, None] < counts[:, None, None]
    )
    picks_f = picks.astype(jnp.float32)
    places = lax.iota(jnp.int32, region).astype(jnp.float32)
    packed = jnp.einsum("nkr,nrd->nkd", picks_f, accum, precision=lax.Precision.HIGHEST)
    where_at = jnp.einsum("nkr,r->nk", picks_f, places, precision=lax.Precision.HIGHEST)
    return (packed, where_at)


def unpack_slots(arrived, spots, region, width):
    places = lax.iota(jnp.int32, region).astype(jnp.float32)
    placed = (spots.reshape(-1)[:, None] == places[None, :]).astype(jnp.float32)
    return jnp.einsum(
        "mr,md->rd", placed, arrived.reshape(-1, width), precision=lax.Precision.HIGHEST
    )


def owner_section(pod_sum, oresid, ranks_out, count_out):
    owner_acc = pod_sum + oresid
    passed = (ranks_out < count_out)[:, None]
    outgoing = jnp.where(passed, owner_acc, jnp.float32(0.0))
    kept = jnp.where(passed, jnp.float32(0.0), owner_acc)
    return (outgoing, kept)


def per_device(acts, cotangent, residual, owner_residual, in_count, in_rank, out_count, out_rank):
    owners = lax.axis_size("inner")
    steps = acts.shape[1]
    tokens = acts.shape[2]
    rows = acts.shape[3]
    cols = cotangent.shape[3]
    blocks = residual.shape[1]
    width = residual.shape[2]
    region = blocks // owners
    slots = max(1, region // 2)
    scale = 1.0 / math.sqrt(tokens * owners)
    resid = residual[0]
    oresid = owner_residual[0]
    crosses = []
    packs = []
    spots_all = []
    for step in range(steps):
        grad = (
            jnp.einsum(
                "tr,tc->rc", acts[0, step], cotangent[0, step], preferred_element_type=jnp.float32
            )
            * scale
        )
        counts = in_count[0, step]
        accum, ranks, chosen, resid = select_blocks(
            resid, grad, in_rank[0, step], counts, owners, region, width
        )
        packed, where_at = pack_slots(accum, ranks, counts, slots, region)
        packs.append(packed)
        spots_all.append(where_at)
    arrived, spots = (
        lax.all_to_all(
            jnp.concatenate(packs, axis=1), "inner", split_axis=0, concat_axis=0, tiled=True
        ),
        lax.all_to_all(
            jnp.concatenate(spots_all, axis=1), "inner", split_axis=0, concat_axis=0, tiled=True
        ),
    )
    outgoings = []
    for step in range(steps):
        pod_sum = unpack_slots(
            arrived[:, step * slots : (step + 1) * slots],
            spots[:, step * slots : (step + 1) * slots],
            region,
            width,
        )
        outgoing, oresid = owner_section(pod_sum, oresid, out_rank[0, step], out_count[0, step])
        outgoings.append(outgoing)
    summed = lax.psum(jnp.stack(outgoings), "outer")
    for step in range(steps):
        crosses.append(summed[step])
    deltas = []
    for cross in crosses:
        delta = cross.astype(jnp.bfloat16)
        deltas.append(lax.all_gather(delta, "inner", axis=0, tiled=True))
    total = deltas[0].astype(jnp.float32)
    for later in deltas[1:]:
        total = total + later.astype(jnp.float32)
    applied = (-step_size * total).astype(jnp.bfloat16)
    return (applied.reshape(rows, cols), resid[None], oresid[None])


LANES = 128
F32 = jnp.float32
BF16 = jnp.bfloat16


def fused_kernel(
    dims,
    acts_hbm, cot_hbm, res_hbm, ores_hbm, cnt_hbm, rank_hbm, ocnt_hbm, orank_hbm,
    ag, resid_ref, nores_ref,
    ores_ref, cnt_ref, rank_ref, ocnt_ref, orank_ref, small_sem,
    acts_v, cot_v, res_v, rk_ref, rp_ref, mt_ref, msend, mrecv, mall_ref, tab_ref,
    sent, psum, tsend, trecv, usend, urecv, osend, orecv, okeep,
    in_sem, ms_sem, mr_sem, ss_sem, sr_sem, ts_sem, tr_sem, us_sem, ur_sem, os_sem, or_sem,
    zs_sem, zr_sem, fs_sem, fr_sem, ps_sem, pr_sem,
):
    n_in, n_out, steps, scale, region, width = dims
    rows, cols = acts_v.shape[2], cot_v.shape[2]
    cpr = cols // width
    rpr = region // cpr
    halves = region // LANES
    rpc = LANES // rpr
    n_z = n_in // 2
    me = lax.axis_index("inner")
    pod = lax.axis_index("outer")
    core = lax.rem(me, 2)
    z = lax.div(me, 2)
    partner = me + 1 - 2 * core

    def outer(d):
        return lax.rem(pod + d, n_out)

    def flip(m):
        v, bit = z, 1
        while bit <= m:
            if m & bit:
                v = v + bit - 2 * bit * lax.rem(lax.div(z, bit), 2)
            bit *= 2
        return v

    def same_core(zz):
        return 2 * zz + core

    far_first = list(range(n_z - 1, 0, -1))

    def remote(src, dst, ssem, rsem, **device):
        return pltpu.make_async_remote_copy(
            src_ref=src, dst_ref=dst, send_sem=ssem, recv_sem=rsem,
            device_id=device, device_id_type=pl.DeviceIdType.MESH,
        )

    sends = []

    def send(*args, **device):
        copy = remote(*args, **device)
        copy.start()
        sends.append(copy)

    def arrive(ref, ssem, rsem, **device):
        remote(ref, ref, ssem, rsem, **device).wait_recv()

    barrier = pltpu.get_barrier_semaphore()
    for m in far_first:
        pl.semaphore_signal(barrier, inc=1, device_id={"inner": same_core(flip(m))}, device_id_type=pl.DeviceIdType.MESH)
    for d in range(1, n_out):
        pl.semaphore_signal(barrier, inc=1, device_id={"outer": outer(d)}, device_id_type=pl.DeviceIdType.MESH)
    pl.semaphore_signal(barrier, inc=1, device_id={"inner": partner}, device_id_type=pl.DeviceIdType.MESH)

    small = [
        pltpu.make_async_copy(src, dst, small_sem.at[k])
        for k, (src, dst) in enumerate(
            ((rank_hbm, rank_ref), (cnt_hbm, cnt_ref), (orank_hbm, orank_ref), (ocnt_hbm, ocnt_ref), (ores_hbm, ores_ref))
        )
    ]
    for copy in small:
        copy.start()
    loads = []
    for s in range(steps):
        pair = [
            pltpu.make_async_copy(acts_hbm.at[s], acts_v.at[s], in_sem.at[2 * s]),
            pltpu.make_async_copy(cot_hbm.at[s], cot_v.at[s], in_sem.at[2 * s + 1]),
        ]
        for copy in pair:
            copy.start()
        loads.append(pair)
        if s == 0:
            res_load = pltpu.make_async_copy(res_hbm, res_v, in_sem.at[2 * steps])
            res_load.start()

    rk_ref[...] = jnp.zeros(rk_ref.shape, F32)
    mall_ref[...] = jnp.zeros(mall_ref.shape, F32)
    msend[...] = jnp.zeros(msend.shape, F32)
    for copy in small:
        copy.wait()
    for s in range(steps):
        for j in range(n_in):
            row = rank_ref[s : s + 1, j * region : (j + 1) * region]
            rk_ref[s * n_in + j : s * n_in + j + 1, :] = jnp.where(row < cnt_ref[s : s + 1, j : j + 1], 1.0, 0.0)
    later = jnp.zeros((1, region), F32)
    for s in reversed(range(steps)):
        later = jnp.where(orank_ref[s : s + 1, :] < ocnt_ref[0:1, s : s + 1], 1.0, later)
        rk_ref[steps * n_in + s : steps * n_in + s + 1, :] = later
    old = lax.broadcasted_iota(jnp.int32, (region, region), 0)
    new = lax.broadcasted_iota(jnp.int32, (region, region), 1)
    shift = rpr.bit_length() - 1
    perm = jnp.where(old == (new & (rpr - 1)) * cpr + (new >> shift), 1.0, 0.0).astype(BF16)
    rp = jnp.dot(rk_ref[...].astype(BF16), perm, preferred_element_type=F32)
    rp_ref[...] = rp

    def eye(n):
        return jnp.where(
            lax.broadcasted_iota(jnp.int32, (n, LANES), 0) == lax.broadcasted_iota(jnp.int32, (n, LANES), 1), 1.0, 0.0
        ).astype(BF16)

    def turned(values):
        return lax.dot_general(
            values.astype(BF16), eye(values.shape[0]), (((0,), (0,)), ((), ())), preferred_element_type=F32
        ).astype(BF16)

    def spread(table, index, n):
        pick = jnp.where(lax.broadcasted_iota(jnp.int32, (LANES, n), 0) == index, 1.0, 0.0).astype(BF16)
        return jnp.dot(table, pick, preferred_element_type=F32)

    mt_ref[...] = turned(rp)
    for s in range(steps):
        for h in range(halves):
            msend[s * halves + h : s * halves + h + 1, :] = rp_ref[
                steps * n_in + s : steps * n_in + s + 1, h * LANES : (h + 1) * LANES
            ]

    def share(s, zz):
        send(sent.at[s, 2 * zz + 1 - core], psum.at[s, zz], ss_sem.at[s, zz], sr_sem.at[s, zz], inner=partner)

    for s in range(steps):
        for copy in loads[s]:
            copy.wait()
        if s == 0:
            res_load.wait()
        for q in range(rows // LANES):
            g = lax.dot_general(
                acts_v[s, :, q * LANES : (q + 1) * LANES], cot_v[s], (((0,), (0,)), ((), ())),
                preferred_element_type=F32,
            ) * scale
            for half in range(rpc):
                j = q * rpc + half
                chosen = spread(mt_ref[...], s * n_in + j, width) > 0.5
                for c in range(cpr):
                    where_at = pl.ds(region * j + c, rpr, stride=cpr)
                    acc = res_v[where_at, :] + g[half * rpr : (half + 1) * rpr, c * width : (c + 1) * width]
                    take = chosen[c * rpr : (c + 1) * rpr]
                    (resid_ref if s == steps - 1 else res_v)[where_at, :] = jnp.where(take, 0.0, acc)
                    sent[s, j, c * rpr : (c + 1) * rpr] = jnp.where(take, acc, 0.0).astype(BF16)
            if s:
                for zz in range(q * rpc // 2, (q + 1) * rpc // 2):
                    share(s, zz)
        if s == 0:
            pl.semaphore_wait(barrier, n_z - 1 + n_out)
            for m in far_first:
                send(msend, mrecv.at[z], ms_sem.at[m], mr_sem.at[z], inner=same_core(flip(m)))
            mrecv[z] = msend[...]
            for zz in range(n_z):
                share(s, zz)

    for m in far_first:
        zz = flip(m)
        arrive(mrecv.at[zz], ms_sem.at[m], mr_sem.at[zz], inner=same_core(zz))
    for zz in range(n_z):
        for s in range(steps):
            for h in range(halves):
                mall_ref[zz * steps + s : zz * steps + s + 1, h * LANES : (h + 1) * LANES] = mrecv[
                    zz, s * halves + h : s * halves + h + 1, :
                ]
    tab_ref[...] = turned(mall_ref[...])
    for s in range(steps):
        for zz in range(n_z):
            arrive(psum.at[s, zz], ss_sem.at[s, zz], sr_sem.at[s, zz], inner=partner)

    for m in far_first + [0]:
        zz = flip(m)
        t = jnp.zeros((region, width), F32)
        o = jnp.zeros((region, width), F32)
        for s in range(steps):
            part = sent[s, same_core(zz)].astype(F32) + psum[s, zz].astype(F32)
            if s == 0 and m == 0:
                part = part + jnp.concatenate([ores_ref[pl.ds(c, rpr, stride=cpr), :] for c in range(cpr)], axis=0)
            passed = spread(tab_ref[...], zz * steps + s, width) > 0.5
            t = t + jnp.where(passed, part, 0.0)
            o = o + jnp.where(passed, 0.0, part)
        for q in range(n_out):
            tsend[zz, q] = t[q * rpr : (q + 1) * rpr].astype(BF16)
        for d in range(1, n_out):
            send(tsend.at[zz, outer(d)], trecv.at[zz, pod], ts_sem.at[m, d], tr_sem.at[zz, pod], outer=outer(d))
        if m:
            osend[zz] = o.astype(BF16)
        else:
            okeep[...] = o
    for m in far_first:
        zz = flip(m)
        send(osend.at[zz], orecv.at[z], os_sem.at[m], or_sem.at[z], inner=same_core(zz))

    for m in far_first + [0]:
        zz = flip(m)
        total = tsend[zz, pod].astype(F32)
        for d in range(1, n_out):
            q = outer(d)
            arrive(trecv.at[zz, q], ts_sem.at[m, d], tr_sem.at[zz, q], outer=q)
            total = total + trecv[zz, q].astype(F32)
        if m:
            usend[zz] = total.astype(BF16)
            send(usend.at[zz], urecv.at[z], us_sem.at[m], ur_sem.at[z], inner=same_core(zz))
    for m in reversed(far_first):
        zz = flip(m)
        arrive(urecv.at[zz], us_sem.at[m], ur_sem.at[zz], inner=same_core(zz))
        total = total + urecv[zz].astype(F32)
    ag[pod, z, core] = (-step_size * total).astype(BF16)

    def forward(m):
        zz = flip(m)
        piece = ag.at[pod, zz, core]
        for d in range(1, n_out):
            send(piece, piece, fs_sem.at[m, d], fr_sem.at[pod, zz], outer=outer(d))

    def hand_over(q, m, d):
        piece = ag.at[q, flip(m), core]
        send(piece, piece, ps_sem.at[m, d], pr_sem.at[q, flip(m)], inner=partner)

    own = ag.at[pod, z, core]
    for m in far_first:
        send(own, own, zs_sem.at[m], zr_sem.at[z], inner=same_core(flip(m)))
    forward(0)
    hand_over(pod, 0, 0)

    kept = okeep[...]
    for m in far_first:
        zz = flip(m)
        arrive(orecv.at[zz], os_sem.at[m], or_sem.at[zz], inner=same_core(zz))
        kept = kept + orecv[zz].astype(F32)
    for c in range(cpr):
        nores_ref[pl.ds(c, rpr, stride=cpr), :] = kept[c * rpr : (c + 1) * rpr]

    for m in reversed(far_first):
        zz = flip(m)
        piece = ag.at[pod, zz, core]
        arrive(piece, zs_sem.at[m], zr_sem.at[zz], inner=same_core(zz))
        forward(m)
        hand_over(pod, m, 0)
    for m in range(n_z):
        for d in range(1, n_out):
            q = outer(d)
            arrive(ag.at[q, flip(m), core], fs_sem.at[m, d], fr_sem.at[q, flip(m)], outer=q)
            hand_over(q, m, d)
    for m in range(n_z):
        for d in range(n_out):
            q = outer(d)
            arrive(ag.at[q, flip(m), 1 - core], ps_sem.at[m, d], pr_sem.at[q, flip(m)], inner=partner)
    for copy in sends:
        copy.wait_send()


def hand_out(pieces, *arrays):
    n = len(arrays)
    pods, rows, width = pieces.shape

    def kernel(*refs):
        src, dst, sems = refs[: n + 1], refs[n + 1 : 2 * n + 2], refs[2 * n + 2]
        copies = [pltpu.make_async_copy(src[k], dst[k], sems.at[k]) for k in range(1, n + 1)]
        copies += [
            pltpu.make_async_copy(src[0].at[q], dst[0].at[:, q * width : (q + 1) * width], sems.at[n + 1 + q])
            for q in range(pods)
        ]
        for copy in copies:
            copy.start()
        for copy in copies:
            copy.wait()

    return pl.pallas_call(
        kernel,
        out_shape=(jax.ShapeDtypeStruct((rows, pods * width), pieces.dtype),)
        + tuple(jax.ShapeDtypeStruct(a.shape, a.dtype) for a in arrays),
        in_specs=[pl.BlockSpec(memory_space=pltpu.VMEM)] * (n + 1),
        out_specs=tuple([pl.BlockSpec(memory_space=pltpu.HBM)] * (n + 1)),
        scratch_shapes=[pltpu.SemaphoreType.DMA((n + 1 + pods,))],
        compiler_params=pltpu.CompilerParams(vmem_limit_bytes=4 << 20),
    )(pieces, *arrays)


def fits(owners, pods, steps, rows, cols, blocks, width, region):
    if width != LANES or region % LANES or region > 256 or cols % width or owners % 4:
        return False
    cpr = cols // width
    rpr = region // cpr
    n_z = owners // 2
    return (
        cpr == pods and cpr * rpr == region and rpr % 16 == 0 and 2 * rpr == LANES
        and rows % LANES == 0 and n_z & (n_z - 1) == 0
        and rpr * owners == rows and steps * (owners + 1) <= LANES and steps * (region // LANES) <= 8
    )


def per_device_fused(acts, cotangent, residual, owner_residual, in_count, in_rank, out_count, out_rank):
    n_in = lax.axis_size("inner")
    n_out = lax.axis_size("outer")
    steps, tokens, rows = acts.shape[1:]
    cols = cotangent.shape[3]
    blocks, width = residual.shape[1:]
    region = blocks // n_in
    if not fits(n_in, n_out, steps, rows, cols, blocks, width, region):
        return per_device(acts, cotangent, residual, owner_residual, in_count, in_rank, out_count, out_rank)
    scale = 1.0 / math.sqrt(tokens * n_in)
    rpr = region // n_out
    n_z = n_in // 2
    n_rk = -(-steps * (n_in + 1) // 16) * 16
    n_ra = -(-steps * n_z // 16) * 16
    vmem = pl.BlockSpec(memory_space=pltpu.VMEM)
    anywhere = pl.BlockSpec(memory_space=pltpu.HBM)
    dma = pltpu.SemaphoreType.DMA
    pieces, resid, oresid = pl.pallas_call(
        functools.partial(fused_kernel, (n_in, n_out, steps, scale, region, width)),
        out_shape=(
            jax.ShapeDtypeStruct((n_out, n_z, 2, rpr, width), BF16),
            jax.ShapeDtypeStruct((blocks, width), F32),
            jax.ShapeDtypeStruct((region, width), F32),
        ),
        in_specs=[anywhere] * 8,
        out_specs=(vmem, vmem, vmem),
        scratch_shapes=[
            pltpu.VMEM((region, width), F32),
            pltpu.VMEM((steps, n_in), jnp.int32),
            pltpu.VMEM((steps, blocks), jnp.int32),
            pltpu.VMEM((1, steps), jnp.int32),
            pltpu.VMEM((steps, region), jnp.int32),
            dma((5,)),
            pltpu.VMEM((steps, tokens, rows), BF16),
            pltpu.VMEM((steps, tokens, cols), BF16),
            pltpu.VMEM((blocks, width), F32),
            pltpu.VMEM((n_rk, region), F32),
            pltpu.VMEM((n_rk, region), F32),
            pltpu.VMEM((region, LANES), BF16),
            pltpu.VMEM((8, LANES), F32),
            pltpu.VMEM((n_z, 8, LANES), F32),
            pltpu.VMEM((n_ra, region), F32),
            pltpu.VMEM((region, LANES), BF16),
            pltpu.VMEM((steps, n_in, region, width), BF16),
            pltpu.VMEM((steps, n_z, region, width), BF16),
            pltpu.VMEM((n_z, n_out, rpr, width), BF16),
            pltpu.VMEM((n_z, n_out, rpr, width), BF16),
            pltpu.VMEM((n_z, rpr, width), BF16),
            pltpu.VMEM((n_z, rpr, width), BF16),
            pltpu.VMEM((n_z, region, width), BF16),
            pltpu.VMEM((n_z, region, width), BF16),
            pltpu.VMEM((region, width), F32),
            dma((2 * steps + 1,)),
            dma((n_z,)),
            dma((n_z,)),
            dma((steps, n_z)),
            dma((steps, n_z)),
            dma((n_z, n_out)),
            dma((n_z, n_out)),
            dma((n_z,)),
            dma((n_z,)),
            dma((n_z,)),
            dma((n_z,)),
            dma((n_z,)),
            dma((n_z,)),
            dma((n_z, n_out)),
            dma((n_out, n_z)),
            dma((n_z, n_out)),
            dma((n_out, n_z)),
        ],
        compiler_params=pltpu.CompilerParams(collective_id=0, has_side_effects=True, vmem_limit_bytes=48 << 20),
    )(*(
        pltpu.with_memory_space_constraint(a, pltpu.HBM)
        for a in (
            acts[0], cotangent[0], residual[0], owner_residual[0], in_count[0], in_rank[0], out_count, out_rank[0]
        )
    ))
    applied, resid, oresid = hand_out(pieces.reshape(n_out, rows, width), resid, oresid)
    return applied, resid[None], oresid[None]


def solution(mesh):
    return jax.shard_map(
        per_device_fused,
        mesh=mesh,
        in_specs=(
            P(("outer", "inner"), None, None, None),
            P(("outer", "inner"), None, None, None),
            P(("outer", "inner"), None, None),
            P(("outer", "inner"), None, None),
            P(("outer", "inner"), None, None),
            P(("outer", "inner"), None, None),
            P(("outer", "inner"), None),
            P(("outer", "inner"), None, None),
        ),
        out_specs=(P(), P(("outer", "inner"), None, None), P(("outer", "inner"), None, None)),
        check_vma=False,
    )
```

time: 33.9 us -> 30.6 us (0.903)
  Pallas kernels: 33 us -> 29.7 us
    pallas_call x1, Pallas kernels: 31.8 us -> 28.5 us  [per_device_fused(): pl.pallas_call(functools.partial(fused_kernel, (n_in, n_out, steps, scale...]
where the time goes in v1:
time: 30.6 us; the launch traced here: 30.4 us
  Pallas kernels  29.7 us (97%)
  between operations  0.64 us (2%)
    pallas_call x1, Pallas kernels, per_device_fused(): pl.pallas_call(functools.partial(fused_kernel, (n_in, n_out, steps, scale...  28.5 us
    pallas_call x1, Pallas kernels, hand_out(): pl.pallas_call(kernel, out_shape=(jax.ShapeDtypeStruct((rows, pods * widt...  1.24 us

profile of v1, /device:TPU:0, one launch (start us, length us, event | category | flops | bytes accessed | tf_op | source)
XLA Modules:
  0.0 30.4 jit_solution(12245810765762676347)
XLA Ops:
  0.6 28.5 %shard_map.103 = (bf16[4,4,2,64,128]{4,3,2,1,0:T(8,128)(2,1)S(1)}, f32[2048,128]{1,0:T(8,128)S(1)}, f32[256,128]{1,0:T(8,128)S(1)}) custom-call(bf16[2,512,512]{2,1,0:T(8,128)(2,1)} %bitcast.11, bf16[2,512,512]{2,1,0:T(8,128)(2,1)} %bitcast.12, f32[2048,128]{1,0:T(8,128)} %bitcast.13, f32[256,128]{1,0:T(8,128)} %bitcast.14, s32[2,8]{1,0:T(2,128)} %bitcast.17, ...), custom_call_target="tpu_custom_call" | custom-call | tf_op jit(solution)/shard_map/pallas_call | solution.py:428
  29.1 1.2 %shard_map.104 = (bf16[512,512]{1,0:T(8,128)(2,1)}, f32[2048,128]{1,0:T(8,128)}, f32[256,128]{1,0:T(8,128)}) custom-call(bf16[4,512,128]{2,1,0:T(8,128)(2,1)S(1)} %bitcast.10, f32[2048,128]{1,0:T(8,128)S(1)} %get-tuple-element.10.refs_1_, f32[256,128]{1,0:T(8,128)S(1)} %get-tuple-element.11.refs_2_), custom_call_target="tpu_custom_call" | custom-call | tf_op jit(solution)/shard_map/pallas_call | solution.py:387

commit v2 on v1

--- a/solution.py
+++ b/solution.py
@@ -119,24 +119,25 @@
     dims,
     acts_hbm, cot_hbm, res_hbm, ores_hbm, cnt_hbm, rank_hbm, ocnt_hbm, orank_hbm,
     ag, resid_ref, nores_ref,
-    ores_ref, cnt_ref, rank_ref, ocnt_ref, orank_ref, small_sem,
+    ores_ref, cnt_ref, rank_ref, ocnt_ref, orank_ref,
     acts_v, cot_v, res_v, rk_ref, rp_ref, mt_ref, msend, mrecv, mall_ref, tab_ref,
     sent, psum, tsend, trecv, usend, urecv, osend, orecv, okeep,
-    in_sem, ms_sem, mr_sem, ss_sem, sr_sem, ts_sem, tr_sem, us_sem, ur_sem, os_sem, or_sem,
-    zs_sem, zr_sem, fs_sem, fr_sem, ps_sem, pr_sem,
+    in_sem, s_sem, g_sem, sr_sem, tr_sem, zr_sem, fr_sem,
 ):
     n_in, n_out, steps, scale, region, width = dims
     rows, cols = acts_v.shape[2], cot_v.shape[2]
     cpr = cols // width
     rpr = region // cpr
     halves = region // LANES
-    rpc = LANES // rpr
+    chunk = 2 * LANES
+    rpc = chunk // rpr
     n_z = n_in // 2
     me = lax.axis_index("inner")
     pod = lax.axis_index("outer")
     core = lax.rem(me, 2)
     z = lax.div(me, 2)
     partner = me + 1 - 2 * core
+    MASK, SHARE, TOTAL, OVER_Z, KEPT, GATHER_Z, GATHER_O, HAND = range(8)
 
     def outer(d):
         return lax.rem(pod + d, n_out)
@@ -160,15 +161,14 @@
             device_id=device, device_id_type=pl.DeviceIdType.MESH,
         )
 
-    sends = []
-
-    def send(*args, **device):
-        copy = remote(*args, **device)
-        copy.start()
-        sends.append(copy)
-
-    def arrive(ref, ssem, rsem, **device):
-        remote(ref, ref, ssem, rsem, **device).wait_recv()
+    def send(phase, src, dst, rsem, **device):
+        remote(src, dst, s_sem.at[phase], rsem, **device).start()
+
+    def arrived(ref, rsem):
+        remote(ref, ref, s_sem.at[0], rsem, inner=partner).wait_recv()
+
+    def left(phase, ref):
+        remote(ref, ref, s_sem.at[phase], g_sem.at[0], inner=partner).wait_send()
 
     barrier = pltpu.get_barrier_semaphore()
     for m in far_first:
@@ -178,7 +178,7 @@
     pl.semaphore_signal(barrier, inc=1, device_id={"inner": partner}, device_id_type=pl.DeviceIdType.MESH)
 
     small = [
-        pltpu.make_async_copy(src, dst, small_sem.at[k])
+        pltpu.make_async_copy(src, dst, in_sem.at[k])
         for k, (src, dst) in enumerate(
             ((rank_hbm, rank_ref), (cnt_hbm, cnt_ref), (orank_hbm, orank_ref), (ocnt_hbm, ocnt_ref), (ores_hbm, ores_ref))
         )
@@ -187,16 +187,15 @@
         copy.start()
     loads = []
     for s in range(steps):
-        pair = [
-            pltpu.make_async_copy(acts_hbm.at[s], acts_v.at[s], in_sem.at[2 * s]),
-            pltpu.make_async_copy(cot_hbm.at[s], cot_v.at[s], in_sem.at[2 * s + 1]),
-        ]
-        for copy in pair:
-            copy.start()
-        loads.append(pair)
+        pltpu.make_async_copy(acts_hbm.at[s], acts_v.at[s], in_sem.at[6 + s]).start()
+        pltpu.make_async_copy(cot_hbm.at[s], cot_v.at[s], in_sem.at[6 + s]).start()
         if s == 0:
-            res_load = pltpu.make_async_copy(res_hbm, res_v, in_sem.at[2 * steps])
+            res_load = pltpu.make_async_copy(res_hbm, res_v, in_sem.at[5])
             res_load.start()
+
+    def loaded(s):
+        both = acts_v.at[0:2]
+        pltpu.make_async_copy(both, both, in_sem.at[6 + s]).wait()
 
     rk_ref[...] = jnp.zeros(rk_ref.shape, F32)
     mall_ref[...] = jnp.zeros(mall_ref.shape, F32)
@@ -232,24 +231,34 @@
         pick = jnp.where(lax.broadcasted_iota(jnp.int32, (LANES, n), 0) == index, 1.0, 0.0).astype(BF16)
         return jnp.dot(table, pick, preferred_element_type=F32)
 
-    mt_ref[...] = turned(rp)
     for s in range(steps):
         for h in range(halves):
             msend[s * halves + h : s * halves + h + 1, :] = rp_ref[
                 steps * n_in + s : steps * n_in + s + 1, h * LANES : (h + 1) * LANES
             ]
+    mt_ref[...] = turned(rp)
+
+    def greet():
+        pl.semaphore_wait(barrier, n_z - 1 + n_out)
+        for m in far_first:
+            send(MASK, msend, mrecv.at[z], g_sem.at[MASK], inner=same_core(flip(m)))
+        mrecv[z] = msend[...]
 
     def share(s, zz):
-        send(sent.at[s, 2 * zz + 1 - core], psum.at[s, zz], ss_sem.at[s, zz], sr_sem.at[s, zz], inner=partner)
-
+        send(SHARE, sent.at[s, 2 * zz + 1 - core], psum.at[s, zz], sr_sem.at[s], inner=partner)
+
+    met = False
+    waiting = []
     for s in range(steps):
-        for copy in loads[s]:
-            copy.wait()
+        if not met and (0, 0) == (s, -1):
+            greet()
+            met = True
+        loaded(s)
         if s == 0:
             res_load.wait()
-        for q in range(rows // LANES):
+        for q in range(rows // chunk):
             g = lax.dot_general(
-                acts_v[s, :, q * LANES : (q + 1) * LANES], cot_v[s], (((0,), (0,)), ((), ())),
+                acts_v[s, :, q * chunk : (q + 1) * chunk], cot_v[s], (((0,), (0,)), ((), ())),
                 preferred_element_type=F32,
             ) * scale
             for half in range(rpc):
@@ -261,20 +270,50 @@
                     take = chosen[c * rpr : (c + 1) * rpr]
                     (resid_ref if s == steps - 1 else res_v)[where_at, :] = jnp.where(take, 0.0, acc)
                     sent[s, j, c * rpr : (c + 1) * rpr] = jnp.where(take, acc, 0.0).astype(BF16)
-            if s:
-                for zz in range(q * rpc // 2, (q + 1) * rpc // 2):
-                    share(s, zz)
-        if s == 0:
-            pl.semaphore_wait(barrier, n_z - 1 + n_out)
-            for m in far_first:
-                send(msend, mrecv.at[z], ms_sem.at[m], mr_sem.at[z], inner=same_core(flip(m)))
-            mrecv[z] = msend[...]
-            for zz in range(n_z):
-                share(s, zz)
-
-    for m in far_first:
+            waiting += [(s, zz) for zz in range(q * rpc // 2, (q + 1) * rpc // 2)]
+            if not met and (0, 0) == (s, q):
+                greet()
+                met = True
+            if met:
+                for pair in waiting:
+                    share(*pair)
+                waiting = []
+
+    for s in range(steps):
+        arrived(psum.at[s], sr_sem.at[s])
+
+    def split(m):
         zz = flip(m)
-        arrive(mrecv.at[zz], ms_sem.at[m], mr_sem.at[zz], inner=same_core(zz))
+        t = jnp.zeros((region, width), F32)
+        o = jnp.zeros((region, width), F32)
+        for s in range(steps):
+            part = sent[s, same_core(zz)].astype(F32) + psum[s, zz].astype(F32)
+            if m:
+                passed = spread(tab_ref[...], zz * steps + s, width) > 0.5
+            else:
+                passed = spread(mt_ref[...], steps * n_in + s, width) > 0.5
+                if s == 0:
+                    part = part + jnp.concatenate([ores_ref[pl.ds(c, rpr, stride=cpr), :] for c in range(cpr)], axis=0)
+            t = t + jnp.where(passed, part, 0.0)
+            o = o + jnp.where(passed, 0.0, part)
+        for q in range(n_out):
+            tsend[zz, q] = t[q * rpr : (q + 1) * rpr].astype(BF16)
+        for d in range(1, n_out):
+            send(TOTAL, tsend.at[zz, outer(d)], trecv.at[zz, pod], tr_sem.at[zz], outer=outer(d))
+        if m:
+            osend[zz] = o.astype(BF16)
+        else:
+            okeep[...] = o
+
+    half = region // 2
+
+    def send_kept(m, k):
+        zz = flip(m)
+        at = pl.ds(k * half, half)
+        send(KEPT, osend.at[zz, at], orecv.at[z, at], g_sem.at[KEPT], inner=same_core(zz))
+
+    split(0)
+    arrived(mrecv.at[0 : n_z - 1], g_sem.at[MASK])
     for zz in range(n_z):
         for s in range(steps):
             for h in range(halves):
@@ -282,90 +321,70 @@
                     zz, s * halves + h : s * halves + h + 1, :
                 ]
     tab_ref[...] = turned(mall_ref[...])
-    for s in range(steps):
-        for zz in range(n_z):
-            arrive(psum.at[s, zz], ss_sem.at[s, zz], sr_sem.at[s, zz], inner=partner)
+    for m in far_first:
+        split(m)
+    late = [(2, 1)]
+    for m in far_first:
+        for k in range(2):
+            if (m, k) not in late:
+                send_kept(m, k)
 
     for m in far_first + [0]:
         zz = flip(m)
-        t = jnp.zeros((region, width), F32)
-        o = jnp.zeros((region, width), F32)
-        for s in range(steps):
-            part = sent[s, same_core(zz)].astype(F32) + psum[s, zz].astype(F32)
-            if s == 0 and m == 0:
-                part = part + jnp.concatenate([ores_ref[pl.ds(c, rpr, stride=cpr), :] for c in range(cpr)], axis=0)
-            passed = spread(tab_ref[...], zz * steps + s, width) > 0.5
-            t = t + jnp.where(passed, part, 0.0)
-            o = o + jnp.where(passed, 0.0, part)
-        for q in range(n_out):
-            tsend[zz, q] = t[q * rpr : (q + 1) * rpr].astype(BF16)
-        for d in range(1, n_out):
-            send(tsend.at[zz, outer(d)], trecv.at[zz, pod], ts_sem.at[m, d], tr_sem.at[zz, pod], outer=outer(d))
-        if m:
-            osend[zz] = o.astype(BF16)
-        else:
-            okeep[...] = o
-    for m in far_first:
-        zz = flip(m)
-        send(osend.at[zz], orecv.at[z], os_sem.at[m], or_sem.at[z], inner=same_core(zz))
-
-    for m in far_first + [0]:
-        zz = flip(m)
+        arrived(trecv.at[zz, 0 : n_out - 1], tr_sem.at[zz])
         total = tsend[zz, pod].astype(F32)
         for d in range(1, n_out):
-            q = outer(d)
-            arrive(trecv.at[zz, q], ts_sem.at[m, d], tr_sem.at[zz, q], outer=q)
-            total = total + trecv[zz, q].astype(F32)
+            total = total + trecv[zz, outer(d)].astype(F32)
         if m:
             usend[zz] = total.astype(BF16)
-            send(usend.at[zz], urecv.at[z], us_sem.at[m], ur_sem.at[z], inner=same_core(zz))
-    for m in reversed(far_first):
-        zz = flip(m)
-        arrive(urecv.at[zz], us_sem.at[m], ur_sem.at[zz], inner=same_core(zz))
-        total = total + urecv[zz].astype(F32)
-    ag[pod, z, core] = (-step_size * total).astype(BF16)
+            send(OVER_Z, usend.at[zz], urecv.at[z], g_sem.at[OVER_Z], inner=same_core(zz))
+    for part in late:
+        send_kept(*part)
+    arrived(urecv.at[0 : n_z - 1], g_sem.at[OVER_Z])
+    for m in far_first:
+        total = total + urecv[flip(m)].astype(F32)
+    own = ag.at[pod, z, core]
+    own[...] = (-step_size * total).astype(BF16)
 
     def forward(m):
         zz = flip(m)
         piece = ag.at[pod, zz, core]
         for d in range(1, n_out):
-            send(piece, piece, fs_sem.at[m, d], fr_sem.at[pod, zz], outer=outer(d))
-
-    def hand_over(q, m, d):
+            send(GATHER_O, piece, piece, fr_sem.at[zz], outer=outer(d))
+
+    def hand_over(q, m):
         piece = ag.at[q, flip(m), core]
-        send(piece, piece, ps_sem.at[m, d], pr_sem.at[q, flip(m)], inner=partner)
-
-    own = ag.at[pod, z, core]
+        send(HAND, piece, piece, g_sem.at[HAND], inner=partner)
+
     for m in far_first:
-        send(own, own, zs_sem.at[m], zr_sem.at[z], inner=same_core(flip(m)))
+        send(GATHER_Z, own, own, zr_sem.at[z], inner=same_core(flip(m)))
     forward(0)
-    hand_over(pod, 0, 0)
-
+    hand_over(pod, 0)
+
+    arrived(orecv.at[0 : n_z - 1], g_sem.at[KEPT])
     kept = okeep[...]
     for m in far_first:
-        zz = flip(m)
-        arrive(orecv.at[zz], os_sem.at[m], or_sem.at[zz], inner=same_core(zz))
-        kept = kept + orecv[zz].astype(F32)
+        kept = kept + orecv[flip(m)].astype(F32)
     for c in range(cpr):
         nores_ref[pl.ds(c, rpr, stride=cpr), :] = kept[c * rpr : (c + 1) * rpr]
 
     for m in reversed(far_first):
-        zz = flip(m)
-        piece = ag.at[pod, zz, core]
-        arrive(piece, zs_sem.at[m], zr_sem.at[zz], inner=same_core(zz))
+        arrived(ag.at[pod, flip(m), core], zr_sem.at[flip(m)])
         forward(m)
-        hand_over(pod, m, 0)
+        hand_over(pod, m)
     for m in range(n_z):
+        arrived(ag.at[0 : n_out - 1, flip(m), core], fr_sem.at[flip(m)])
         for d in range(1, n_out):
-            q = outer(d)
-            arrive(ag.at[q, flip(m), core], fs_sem.at[m, d], fr_sem.at[q, flip(m)], outer=q)
-            hand_over(q, m, d)
-    for m in range(n_z):
-        for d in range(n_out):
-            q = outer(d)
-            arrive(ag.at[q, flip(m), 1 - core], ps_sem.at[m, d], pr_sem.at[q, flip(m)], inner=partner)
-    for copy in sends:
-        copy.wait_send()
+            hand_over(outer(d), m)
+    arrived(ag.at[:, :, 1 - core], g_sem.at[HAND])
+    left(MASK, mrecv.at[0 : n_z - 1])
+    left(SHARE, psum)
+    left(TOTAL, trecv.at[:, 0 : n_out - 1])
+    left(OVER_Z, urecv.at[0 : n_z - 1])
+    left(KEPT, orecv.at[0 : n_z - 1])
+    left(GATHER_Z, urecv.at[0 : n_z - 1])
+    left(GATHER_O, trecv.at[:, 0 : n_out - 1])
+    left(HAND, trecv)
 
 
 def hand_out(pieces, *arrays):
@@ -440,7 +459,6 @@
             pltpu.VMEM((steps, blocks), jnp.int32),
             pltpu.VMEM((1, steps), jnp.int32),
             pltpu.VMEM((steps, region), jnp.int32),
-            dma((5,)),
             pltpu.VMEM((steps, tokens, rows), BF16),
             pltpu.VMEM((steps, tokens, cols), BF16),
             pltpu.VMEM((blocks, width), F32),
@@ -460,23 +478,13 @@
             pltpu.VMEM((n_z, region, width), BF16),
             pltpu.VMEM((n_z, region, width), BF16),
             pltpu.VMEM((region, width), F32),
-            dma((2 * steps + 1,)),
-            dma((n_z,)),
-            dma((n_z,)),
-            dma((steps, n_z)),
-            dma((steps, n_z)),
-            dma((n_z, n_out)),
-            dma((n_z, n_out)),
+            dma((6 + steps,)),
+            dma((8,)),
+            dma((8,)),
+            dma((steps,)),
             dma((n_z,)),
             dma((n_z,)),
             dma((n_z,)),
-            dma((n_z,)),
-            dma((n_z,)),
-            dma((n_z,)),
-            dma((n_z, n_out)),
-            dma((n_out, n_z)),
-            dma((n_z, n_out)),
-            dma((n_out, n_z)),
         ],
         compiler_params=pltpu.CompilerParams(collective_id=0, has_side_effects=True, vmem_limit_bytes=48 << 20),
     )(*(

time: 30.6 us -> 28.7 us (0.938)
  Pallas kernels: 29.7 us -> 27.9 us
    pallas_call x1, Pallas kernels: 28.5 us -> 26.6 us  [per_device_fused(): pl.pallas_call(functools.partial(fused_kernel, (n_in, n_out, steps, scale...]
where the time goes in v2:
time: 28.7 us; the launch traced here: 28.5 us
  Pallas kernels  27.9 us (97%)
  between operations  0.64 us (2%)
    pallas_call x1, Pallas kernels, per_device_fused(): pl.pallas_call(functools.partial(fused_kernel, (n_in, n_out, steps, scale...  26.6 us
    pallas_call x1, Pallas kernels, hand_out(): pl.pallas_call(kernel, out_shape=(jax.ShapeDtypeStruct((rows, pods * widt...  1.24 us

profile of v2, /device:TPU:0, one launch (start us, length us, event | category | flops | bytes accessed | tf_op | source)
XLA Modules:
  0.0 28.5 jit_solution(5602115866828802095)
XLA Ops:
  0.6 26.6 %shard_map.103 = (bf16[4,4,2,64,128]{4,3,2,1,0:T(8,128)(2,1)S(1)}, f32[2048,128]{1,0:T(8,128)S(1)}, f32[256,128]{1,0:T(8,128)S(1)}) custom-call(bf16[2,512,512]{2,1,0:T(8,128)(2,1)} %bitcast.11, bf16[2,512,512]{2,1,0:T(8,128)(2,1)} %bitcast.12, f32[2048,128]{1,0:T(8,128)} %bitcast.13, f32[256,128]{1,0:T(8,128)} %bitcast.14, s32[2,8]{1,0:T(2,128)} %bitcast.17, ...), custom_call_target="tpu_custom_call" | custom-call | tf_op jit(solution)/shard_map/pallas_call | solution.py:447
  27.3 1.2 %shard_map.104 = (bf16[512,512]{1,0:T(8,128)(2,1)}, f32[2048,128]{1,0:T(8,128)}, f32[256,128]{1,0:T(8,128)}) custom-call(bf16[4,512,128]{2,1,0:T(8,128)(2,1)S(1)} %bitcast.10, f32[2048,128]{1,0:T(8,128)S(1)} %get-tuple-element.10.refs_1_, f32[256,128]{1,0:T(8,128)S(1)} %get-tuple-element.11.refs_2_), custom_call_target="tpu_custom_call" | custom-call | tf_op jit(solution)/shard_map/pallas_call | solution.py:406

commit v3 on v2

--- a/solution.py
+++ b/solution.py
@@ -120,9 +120,9 @@
     acts_hbm, cot_hbm, res_hbm, ores_hbm, cnt_hbm, rank_hbm, ocnt_hbm, orank_hbm,
     ag, resid_ref, nores_ref,
     ores_ref, cnt_ref, rank_ref, ocnt_ref, orank_ref,
-    acts_v, cot_v, res_v, rk_ref, rp_ref, mt_ref, msend, mrecv, mall_ref, tab_ref,
+    acts_v, cot_v, res_v, rk_ref, rp_ref, mt_ref, msend, mrecv,
     sent, psum, tsend, trecv, usend, urecv, osend, orecv, okeep,
-    in_sem, s_sem, g_sem, sr_sem, tr_sem, zr_sem, fr_sem,
+    in_sem, s_sem, g_sem, mr_sem, sr_sem, tr_sem, zr_sem, fr_sem,
 ):
     n_in, n_out, steps, scale, region, width = dims
     rows, cols = acts_v.shape[2], cot_v.shape[2]
@@ -137,7 +137,7 @@
     core = lax.rem(me, 2)
     z = lax.div(me, 2)
     partner = me + 1 - 2 * core
-    MASK, SHARE, TOTAL, OVER_Z, KEPT, GATHER_Z, GATHER_O, HAND = range(8)
+    OVER_Z, KEPT, HAND, MASK, SHARE, TOTAL, GATHER_Z, GATHER_O = range(8)
 
     def outer(d):
         return lax.rem(pod + d, n_out)
@@ -185,23 +185,25 @@
     ]
     for copy in small:
         copy.start()
-    loads = []
-    for s in range(steps):
+
+    def fetch(s):
         pltpu.make_async_copy(acts_hbm.at[s], acts_v.at[s], in_sem.at[6 + s]).start()
         pltpu.make_async_copy(cot_hbm.at[s], cot_v.at[s], in_sem.at[6 + s]).start()
-        if s == 0:
-            res_load = pltpu.make_async_copy(res_hbm, res_v, in_sem.at[5])
-            res_load.start()
+
+    fetch(0)
+    res_load = pltpu.make_async_copy(res_hbm, res_v, in_sem.at[5])
+    res_load.start()
 
     def loaded(s):
         both = acts_v.at[0:2]
         pltpu.make_async_copy(both, both, in_sem.at[6 + s]).wait()
 
     rk_ref[...] = jnp.zeros(rk_ref.shape, F32)
-    mall_ref[...] = jnp.zeros(mall_ref.shape, F32)
     msend[...] = jnp.zeros(msend.shape, F32)
     for copy in small:
         copy.wait()
+    for s in range(1, steps):
+        fetch(s)
     for s in range(steps):
         for j in range(n_in):
             row = rank_ref[s : s + 1, j * region : (j + 1) * region]
@@ -241,8 +243,7 @@
     def greet():
         pl.semaphore_wait(barrier, n_z - 1 + n_out)
         for m in far_first:
-            send(MASK, msend, mrecv.at[z], g_sem.at[MASK], inner=same_core(flip(m)))
-        mrecv[z] = msend[...]
+            send(MASK, msend, mrecv.at[z], mr_sem.at[z], inner=same_core(flip(m)))
 
     def share(s, zz):
         send(SHARE, sent.at[s, 2 * zz + 1 - core], psum.at[s, zz], sr_sem.at[s], inner=partner)
@@ -250,7 +251,7 @@
     met = False
     waiting = []
     for s in range(steps):
-        if not met and (0, 0) == (s, -1):
+        if not met and (0, 1) == (s, -1):
             greet()
             met = True
         loaded(s)
@@ -271,7 +272,7 @@
                     (resid_ref if s == steps - 1 else res_v)[where_at, :] = jnp.where(take, 0.0, acc)
                     sent[s, j, c * rpr : (c + 1) * rpr] = jnp.where(take, acc, 0.0).astype(BF16)
             waiting += [(s, zz) for zz in range(q * rpc // 2, (q + 1) * rpc // 2)]
-            if not met and (0, 0) == (s, q):
+            if not met and (0, 1) == (s, q):
                 greet()
                 met = True
             if met:
@@ -282,54 +283,51 @@
     for s in range(steps):
         arrived(psum.at[s], sr_sem.at[s])
 
-    def split(m):
+    def passed(m, s):
+        if m == 0:
+            return spread(mt_ref[...], steps * n_in + s, width) > 0.5
+        rows_of = mrecv[flip(m)].astype(BF16)
+        parts = []
+        for h in range(halves):
+            pick = jnp.where(lax.broadcasted_iota(jnp.int32, (16, width), 0) == s * halves + h, 1.0, 0.0).astype(BF16)
+            parts.append(lax.dot_general(rows_of, pick, (((0,), (0,)), ((), ())), preferred_element_type=F32))
+        return jnp.concatenate(parts, axis=0) > 0.5
+
+    def chip_sum(m, s):
+        part = sent[s, same_core(flip(m))].astype(F32) + psum[s, flip(m)].astype(F32)
+        if m == 0 and s == 0:
+            part = part + jnp.concatenate([ores_ref[pl.ds(c, rpr, stride=cpr), :] for c in range(cpr)], axis=0)
+        return part
+
+    def send_total(m):
         zz = flip(m)
         t = jnp.zeros((region, width), F32)
-        o = jnp.zeros((region, width), F32)
         for s in range(steps):
-            part = sent[s, same_core(zz)].astype(F32) + psum[s, zz].astype(F32)
-            if m:
-                passed = spread(tab_ref[...], zz * steps + s, width) > 0.5
-            else:
-                passed = spread(mt_ref[...], steps * n_in + s, width) > 0.5
-                if s == 0:
-                    part = part + jnp.concatenate([ores_ref[pl.ds(c, rpr, stride=cpr), :] for c in range(cpr)], axis=0)
-            t = t + jnp.where(passed, part, 0.0)
-            o = o + jnp.where(passed, 0.0, part)
+            t = t + jnp.where(passed(m, s), chip_sum(m, s), 0.0)
         for q in range(n_out):
             tsend[zz, q] = t[q * rpr : (q + 1) * rpr].astype(BF16)
         for d in range(1, n_out):
             send(TOTAL, tsend.at[zz, outer(d)], trecv.at[zz, pod], tr_sem.at[zz], outer=outer(d))
-        if m:
-            osend[zz] = o.astype(BF16)
-        else:
-            okeep[...] = o
-
-    half = region // 2
-
-    def send_kept(m, k):
-        zz = flip(m)
-        at = pl.ds(k * half, half)
-        send(KEPT, osend.at[zz, at], orecv.at[z, at], g_sem.at[KEPT], inner=same_core(zz))
-
-    split(0)
-    arrived(mrecv.at[0 : n_z - 1], g_sem.at[MASK])
-    for zz in range(n_z):
+
+    def keep(m):
+        o = jnp.zeros((region, width), F32)
         for s in range(steps):
-            for h in range(halves):
-                mall_ref[zz * steps + s : zz * steps + s + 1, h * LANES : (h + 1) * LANES] = mrecv[
-                    zz, s * halves + h : s * halves + h + 1, :
-                ]
-    tab_ref[...] = turned(mall_ref[...])
-    for m in far_first:
-        split(m)
-    late = [(2, 1)]
-    for m in far_first:
-        for k in range(2):
-            if (m, k) not in late:
-                send_kept(m, k)
-
-    for m in far_first + [0]:
+            o = o + jnp.where(passed(m, s), 0.0, chip_sum(m, s))
+        return o
+
+    def send_kept(m):
+        osend[flip(m)] = keep(m).astype(BF16)
+        send(KEPT, osend.at[flip(m)], orecv.at[z], g_sem.at[KEPT], inner=same_core(flip(m)))
+
+    send_total(0)
+    for m in (1, 2, 3):
+        arrived(mrecv.at[flip(m)], mr_sem.at[flip(m)])
+        send_total(m)
+    for m in (3, 1):
+        send_kept(m)
+    okeep[...] = keep(0)
+
+    for m in (1, 2, 3) + (0,):
         zz = flip(m)
         arrived(trecv.at[zz, 0 : n_out - 1], tr_sem.at[zz])
         total = tsend[zz, pod].astype(F32)
@@ -338,8 +336,6 @@
         if m:
             usend[zz] = total.astype(BF16)
             send(OVER_Z, usend.at[zz], urecv.at[z], g_sem.at[OVER_Z], inner=same_core(zz))
-    for part in late:
-        send_kept(*part)
     arrived(urecv.at[0 : n_z - 1], g_sem.at[OVER_Z])
     for m in far_first:
         total = total + urecv[flip(m)].astype(F32)
@@ -360,13 +356,8 @@
         send(GATHER_Z, own, own, zr_sem.at[z], inner=same_core(flip(m)))
     forward(0)
     hand_over(pod, 0)
-
-    arrived(orecv.at[0 : n_z - 1], g_sem.at[KEPT])
-    kept = okeep[...]
-    for m in far_first:
-        kept = kept + orecv[flip(m)].astype(F32)
-    for c in range(cpr):
-        nores_ref[pl.ds(c, rpr, stride=cpr), :] = kept[c * rpr : (c + 1) * rpr]
+    for m in (2,):
+        send_kept(m)
 
     for m in reversed(far_first):
         arrived(ag.at[pod, flip(m), core], zr_sem.at[flip(m)])
@@ -376,6 +367,13 @@
         arrived(ag.at[0 : n_out - 1, flip(m), core], fr_sem.at[flip(m)])
         for d in range(1, n_out):
             hand_over(outer(d), m)
+    arrived(orecv.at[0 : n_z - 1], g_sem.at[KEPT])
+    kept = okeep[...]
+    for m in far_first:
+        kept = kept + orecv[flip(m)].astype(F32)
+    for c in range(cpr):
+        nores_ref[pl.ds(c, rpr, stride=cpr), :] = kept[c * rpr : (c + 1) * rpr]
+
     arrived(ag.at[:, :, 1 - core], g_sem.at[HAND])
     left(MASK, mrecv.at[0 : n_z - 1])
     left(SHARE, psum)
@@ -440,7 +438,6 @@
     rpr = region // n_out
     n_z = n_in // 2
     n_rk = -(-steps * (n_in + 1) // 16) * 16
-    n_ra = -(-steps * n_z // 16) * 16
     vmem = pl.BlockSpec(memory_space=pltpu.VMEM)
     anywhere = pl.BlockSpec(memory_space=pltpu.HBM)
     dma = pltpu.SemaphoreType.DMA
@@ -465,10 +462,8 @@
             pltpu.VMEM((n_rk, region), F32),
             pltpu.VMEM((n_rk, region), F32),
             pltpu.VMEM((region, LANES), BF16),
-            pltpu.VMEM((8, LANES), F32),
-            pltpu.VMEM((n_z, 8, LANES), F32),
-            pltpu.VMEM((n_ra, region), F32),
-            pltpu.VMEM((region, LANES), BF16),
+            pltpu.VMEM((16, LANES), F32),
+            pltpu.VMEM((n_z, 16, LANES), F32),
             pltpu.VMEM((steps, n_in, region, width), BF16),
             pltpu.VMEM((steps, n_z, region, width), BF16),
             pltpu.VMEM((n_z, n_out, rpr, width), BF16),
@@ -480,7 +475,8 @@
             pltpu.VMEM((region, width), F32),
             dma((6 + steps,)),
             dma((8,)),
-            dma((8,)),
+            dma((3,)),
+            dma((n_z,)),
             dma((steps,)),
             dma((n_z,)),
             dma((n_z,)),

time: 28.7 us -> 26.9 us (0.937)
  Pallas kernels: 27.9 us -> 26 us
    pallas_call x1, Pallas kernels: 26.6 us -> 24.8 us  [per_device_fused(): pl.pallas_call(functools.partial(fused_kernel, (n_in, n_out, steps, scale...]
where the time goes in v3:
time: 26.9 us; the launch traced here: 26.6 us
  Pallas kernels  26 us (97%)
  between operations  0.64 us (2%)
    pallas_call x1, Pallas kernels, per_device_fused(): pl.pallas_call(functools.partial(fused_kernel, (n_in, n_out, steps, scale...  24.8 us
    pallas_call x1, Pallas kernels, hand_out(): pl.pallas_call(kernel, out_shape=(jax.ShapeDtypeStruct((rows, pods * widt...  1.24 us

profile of v3, /device:TPU:0, one launch (start us, length us, event | category | flops | bytes accessed | tf_op | source)
XLA Modules:
  0.0 26.6 jit_solution(9741600778996117478)
XLA Ops:
  0.6 24.8 %shard_map.103 = (bf16[4,4,2,64,128]{4,3,2,1,0:T(8,128)(2,1)S(1)}, f32[2048,128]{1,0:T(8,128)S(1)}, f32[256,128]{1,0:T(8,128)S(1)}) custom-call(bf16[2,512,512]{2,1,0:T(8,128)(2,1)} %bitcast.11, bf16[2,512,512]{2,1,0:T(8,128)(2,1)} %bitcast.12, f32[2048,128]{1,0:T(8,128)} %bitcast.13, f32[256,128]{1,0:T(8,128)} %bitcast.14, s32[2,8]{1,0:T(2,128)} %bitcast.17, ...), custom_call_target="tpu_custom_call" | custom-call | tf_op jit(solution)/shard_map/pallas_call | solution.py:444
  25.4 1.2 %shard_map.104 = (bf16[512,512]{1,0:T(8,128)(2,1)}, f32[2048,128]{1,0:T(8,128)}, f32[256,128]{1,0:T(8,128)}) custom-call(bf16[4,512,128]{2,1,0:T(8,128)(2,1)S(1)} %bitcast.10, f32[2048,128]{1,0:T(8,128)S(1)} %get-tuple-element.10.refs_1_, f32[256,128]{1,0:T(8,128)S(1)} %get-tuple-element.11.refs_2_), custom_call_target="tpu_custom_call" | custom-call | tf_op jit(solution)/shard_map/pallas_call | solution.py:404

commit v4 on v3

--- a/solution.py
+++ b/solution.py
@@ -122,7 +122,7 @@
     ores_ref, cnt_ref, rank_ref, ocnt_ref, orank_ref,
     acts_v, cot_v, res_v, rk_ref, rp_ref, mt_ref, msend, mrecv,
     sent, psum, tsend, trecv, usend, urecv, osend, orecv, okeep,
-    in_sem, s_sem, g_sem, mr_sem, sr_sem, tr_sem, zr_sem, fr_sem,
+    sent_bytes, in_sem, s_sem, g_sem, mr_sem, sr_sem, tr_sem, zr_sem, fr_sem,
 ):
     n_in, n_out, steps, scale, region, width = dims
     rows, cols = acts_v.shape[2], cot_v.shape[2]
@@ -139,21 +139,25 @@
     partner = me + 1 - 2 * core
     OVER_Z, KEPT, HAND, MASK, SHARE, TOTAL, GATHER_Z, GATHER_O = range(8)
 
-    def outer(d):
-        return lax.rem(pod + d, n_out)
-
-    def flip(m):
-        v, bit = z, 1
+    def flipped(at, m):
+        v, bit = at, 1
         while bit <= m:
             if m & bit:
-                v = v + bit - 2 * bit * lax.rem(lax.div(z, bit), 2)
+                v = v + bit - 2 * bit * lax.rem(lax.div(at, bit), 2)
             bit *= 2
         return v
 
+    def flip(m):
+        return flipped(z, m)
+
+    def outer(d):
+        return flipped(pod, d)
+
     def same_core(zz):
         return 2 * zz + core
 
     far_first = list(range(n_z - 1, 0, -1))
+    far_pods = list(range(n_out - 1, 0, -1))
 
     def remote(src, dst, ssem, rsem, **device):
         return pltpu.make_async_remote_copy(
@@ -162,19 +166,20 @@
         )
 
     def send(phase, src, dst, rsem, **device):
-        remote(src, dst, s_sem.at[phase], rsem, **device).start()
+        remote(src, dst, s_sem.at[0], rsem, **device).start()
 
     def arrived(ref, rsem):
         remote(ref, ref, s_sem.at[0], rsem, inner=partner).wait_recv()
 
     def left(phase, ref):
-        remote(ref, ref, s_sem.at[phase], g_sem.at[0], inner=partner).wait_send()
+        remote(ref, ref, s_sem.at[0], g_sem.at[0], inner=partner).wait_send()
 
     barrier = pltpu.get_barrier_semaphore()
     for m in far_first:
         pl.semaphore_signal(barrier, inc=1, device_id={"inner": same_core(flip(m))}, device_id_type=pl.DeviceIdType.MESH)
-    for d in range(1, n_out):
+    for d in far_pods:
         pl.semaphore_signal(barrier, inc=1, device_id={"outer": outer(d)}, device_id_type=pl.DeviceIdType.MESH)
+        pl.semaphore_signal(barrier, inc=1, device_id={"outer": outer(d), "inner": partner}, device_id_type=pl.DeviceIdType.MESH)
     pl.semaphore_signal(barrier, inc=1, device_id={"inner": partner}, device_id_type=pl.DeviceIdType.MESH)
 
     small = [
@@ -241,9 +246,9 @@
     mt_ref[...] = turned(rp)
 
     def greet():
-        pl.semaphore_wait(barrier, n_z - 1 + n_out)
+        pl.semaphore_wait(barrier, n_z - 1 + n_out + n_out - 1)
         for m in far_first:
-            send(MASK, msend, mrecv.at[z], mr_sem.at[z], inner=same_core(flip(m)))
+            send(MASK, msend, mrecv.at[z], mr_sem.at[m - 1], inner=same_core(flip(m)))
 
     def share(s, zz):
         send(SHARE, sent.at[s, 2 * zz + 1 - core], psum.at[s, zz], sr_sem.at[s], inner=partner)
@@ -251,9 +256,6 @@
     met = False
     waiting = []
     for s in range(steps):
-        if not met and (0, 1) == (s, -1):
-            greet()
-            met = True
         loaded(s)
         if s == 0:
             res_load.wait()
@@ -272,7 +274,7 @@
                     (resid_ref if s == steps - 1 else res_v)[where_at, :] = jnp.where(take, 0.0, acc)
                     sent[s, j, c * rpr : (c + 1) * rpr] = jnp.where(take, acc, 0.0).astype(BF16)
             waiting += [(s, zz) for zz in range(q * rpc // 2, (q + 1) * rpc // 2)]
-            if not met and (0, 1) == (s, q):
+            if s == 0 and q == rows // chunk - 1:
                 greet()
                 met = True
             if met:
@@ -306,8 +308,8 @@
             t = t + jnp.where(passed(m, s), chip_sum(m, s), 0.0)
         for q in range(n_out):
             tsend[zz, q] = t[q * rpr : (q + 1) * rpr].astype(BF16)
-        for d in range(1, n_out):
-            send(TOTAL, tsend.at[zz, outer(d)], trecv.at[zz, pod], tr_sem.at[zz], outer=outer(d))
+        for d in far_pods:
+            send(TOTAL, tsend.at[zz, outer(d)], trecv.at[zz, pod], tr_sem.at[m], outer=outer(d))
 
     def keep(m):
         o = jnp.zeros((region, width), F32)
@@ -320,18 +322,20 @@
         send(KEPT, osend.at[flip(m)], orecv.at[z], g_sem.at[KEPT], inner=same_core(flip(m)))
 
     send_total(0)
-    for m in (1, 2, 3):
-        arrived(mrecv.at[flip(m)], mr_sem.at[flip(m)])
+    for m in reversed(far_first):
+        arrived(mrecv.at[flip(m)], mr_sem.at[m - 1])
         send_total(m)
-    for m in (3, 1):
-        send_kept(m)
+    late = n_z // 2
+    for m in far_first:
+        if m != late:
+            send_kept(m)
     okeep[...] = keep(0)
 
-    for m in (1, 2, 3) + (0,):
+    for m in far_first[::-1] + [0]:
         zz = flip(m)
-        arrived(trecv.at[zz, 0 : n_out - 1], tr_sem.at[zz])
+        arrived(trecv.at[zz, 0 : n_out - 1], tr_sem.at[m])
         total = tsend[zz, pod].astype(F32)
-        for d in range(1, n_out):
+        for d in far_pods:
             total = total + trecv[zz, outer(d)].astype(F32)
         if m:
             usend[zz] = total.astype(BF16)
@@ -345,28 +349,30 @@
     def forward(m):
         zz = flip(m)
         piece = ag.at[pod, zz, core]
-        for d in range(1, n_out):
-            send(GATHER_O, piece, piece, fr_sem.at[zz], outer=outer(d))
+        for d in far_pods:
+            send(GATHER_O, piece, piece, fr_sem.at[m], outer=outer(d))
+            if m == n_z - 1:
+                send(GATHER_O, piece, piece, g_sem.at[HAND], outer=outer(d), inner=partner)
 
     def hand_over(q, m):
         piece = ag.at[q, flip(m), core]
         send(HAND, piece, piece, g_sem.at[HAND], inner=partner)
 
     for m in far_first:
-        send(GATHER_Z, own, own, zr_sem.at[z], inner=same_core(flip(m)))
+        send(GATHER_Z, own, own, zr_sem.at[m - 1], inner=same_core(flip(m)))
     forward(0)
     hand_over(pod, 0)
-    for m in (2,):
-        send_kept(m)
+    send_kept(late)
 
     for m in reversed(far_first):
-        arrived(ag.at[pod, flip(m), core], zr_sem.at[flip(m)])
+        arrived(ag.at[pod, flip(m), core], zr_sem.at[m - 1])
         forward(m)
         hand_over(pod, m)
     for m in range(n_z):
-        arrived(ag.at[0 : n_out - 1, flip(m), core], fr_sem.at[flip(m)])
-        for d in range(1, n_out):
-            hand_over(outer(d), m)
+        arrived(ag.at[0 : n_out - 1, flip(m), core], fr_sem.at[m])
+        for d in far_pods:
+            if m < n_z - 1:
+                hand_over(outer(d), m)
     arrived(orecv.at[0 : n_z - 1], g_sem.at[KEPT])
     kept = okeep[...]
     for m in far_first:
@@ -375,14 +381,7 @@
         nores_ref[pl.ds(c, rpr, stride=cpr), :] = kept[c * rpr : (c + 1) * rpr]
 
     arrived(ag.at[:, :, 1 - core], g_sem.at[HAND])
-    left(MASK, mrecv.at[0 : n_z - 1])
-    left(SHARE, psum)
-    left(TOTAL, trecv.at[:, 0 : n_out - 1])
-    left(OVER_Z, urecv.at[0 : n_z - 1])
-    left(KEPT, orecv.at[0 : n_z - 1])
-    left(GATHER_Z, urecv.at[0 : n_z - 1])
-    left(GATHER_O, trecv.at[:, 0 : n_out - 1])
-    left(HAND, trecv)
+    left(0, sent_bytes)
 
 
 def hand_out(pieces, *arrays):
@@ -419,8 +418,8 @@
     rpr = region // cpr
     n_z = owners // 2
     return (
-        cpr == pods and cpr * rpr == region and rpr % 16 == 0 and 2 * rpr == LANES
-        and rows % LANES == 0 and n_z & (n_z - 1) == 0
+        cpr == pods and steps >= 2 and rows == cols and cpr * rpr == region and rpr % 16 == 0 and 2 * rpr == LANES
+        and rows % (2 * LANES) == 0 and n_z & (n_z - 1) == 0 and pods & (pods - 1) == 0
         and rpr * owners == rows and steps * (owners + 1) <= LANES and steps * (region // LANES) <= 8
     )
 
@@ -438,6 +437,9 @@
     rpr = region // n_out
     n_z = n_in // 2
     n_rk = -(-steps * (n_in + 1) // 16) * 16
+    piece = rpr // 2
+    n_sent = (n_z - 1) * (16 + 2 * piece + region // 2) + steps * n_z * region // 2
+    n_sent += 2 * n_z * (n_out - 1) * piece + n_z * n_out * piece
     vmem = pl.BlockSpec(memory_space=pltpu.VMEM)
     anywhere = pl.BlockSpec(memory_space=pltpu.HBM)
     dma = pltpu.SemaphoreType.DMA
@@ -473,13 +475,14 @@
             pltpu.VMEM((n_z, region, width), BF16),
             pltpu.VMEM((n_z, region, width), BF16),
             pltpu.VMEM((region, width), F32),
+            pltpu.VMEM((n_sent, LANES), F32),
             dma((6 + steps,)),
-            dma((8,)),
+            dma((1,)),
             dma((3,)),
-            dma((n_z,)),
+            dma((n_z - 1,)),
             dma((steps,)),
             dma((n_z,)),
-            dma((n_z,)),
+            dma((n_z - 1,)),
             dma((n_z,)),
         ],
         compiler_params=pltpu.CompilerParams(collective_id=0, has_side_effects=True, vmem_limit_bytes=48 << 20),

time: 26.9 us -> 26.1 us (0.970)
  Pallas kernels: 26 us -> 25.2 us
    pallas_call x1, Pallas kernels: 24.8 us -> 24 us  [per_device_fused(): pl.pallas_call(functools.partial(fused_kernel, (n_in, n_out, steps, scale...]
where the time goes in v4:
time: 26.1 us; the launch traced here: 25.9 us
  Pallas kernels  25.2 us (97%)
  between operations  0.64 us (2%)
    pallas_call x1, Pallas kernels, per_device_fused(): pl.pallas_call(functools.partial(fused_kernel, (n_in, n_out, steps, scale...  24 us
    pallas_call x1, Pallas kernels, hand_out(): pl.pallas_call(kernel, out_shape=(jax.ShapeDtypeStruct((rows, pods * widt...  1.24 us

profile of v4, /device:TPU:0, one launch (start us, length us, event | category | flops | bytes accessed | tf_op | source)
XLA Modules:
  0.0 25.9 jit_solution(3017760271394894110)
XLA Ops:
  0.6 24.0 %shard_map.103 = (bf16[4,4,2,64,128]{4,3,2,1,0:T(8,128)(2,1)S(1)}, f32[2048,128]{1,0:T(8,128)S(1)}, f32[256,128]{1,0:T(8,128)S(1)}) custom-call(bf16[2,512,512]{2,1,0:T(8,128)(2,1)} %bitcast.11, bf16[2,512,512]{2,1,0:T(8,128)(2,1)} %bitcast.12, f32[2048,128]{1,0:T(8,128)} %bitcast.13, f32[256,128]{1,0:T(8,128)} %bitcast.14, s32[2,8]{1,0:T(2,128)} %bitcast.17, ...), custom_call_target="tpu_custom_call" | custom-call | tf_op jit(solution)/shard_map/pallas_call | solution.py:446
  24.6 1.2 %shard_map.104 = (bf16[512,512]{1,0:T(8,128)(2,1)}, f32[2048,128]{1,0:T(8,128)}, f32[256,128]{1,0:T(8,128)}) custom-call(bf16[4,512,128]{2,1,0:T(8,128)(2,1)S(1)} %bitcast.10, f32[2048,128]{1,0:T(8,128)S(1)} %get-tuple-element.10.refs_1_, f32[256,128]{1,0:T(8,128)S(1)} %get-tuple-element.11.refs_2_), custom_call_target="tpu_custom_call" | custom-call | tf_op jit(solution)/shard_map/pallas_call | solution.py:403

commit v5 on v4

--- a/solution.py
+++ b/solution.py
@@ -122,7 +122,7 @@
     ores_ref, cnt_ref, rank_ref, ocnt_ref, orank_ref,
     acts_v, cot_v, res_v, rk_ref, rp_ref, mt_ref, msend, mrecv,
     sent, psum, tsend, trecv, usend, urecv, osend, orecv, okeep,
-    sent_bytes, in_sem, s_sem, g_sem, mr_sem, sr_sem, tr_sem, zr_sem, fr_sem,
+    chosen_ref, sent_bytes, in_sem, s_sem, g_sem, mr_sem, sr_sem, tr_sem, zr_sem, fr_sem,
 ):
     n_in, n_out, steps, scale, region, width = dims
     rows, cols = acts_v.shape[2], cot_v.shape[2]
@@ -244,6 +244,8 @@
                 steps * n_in + s : steps * n_in + s + 1, h * LANES : (h + 1) * LANES
             ]
     mt_ref[...] = turned(rp)
+    for r in range(steps * n_in):
+        chosen_ref[r] = spread(mt_ref[...], r, width)
 
     def greet():
         pl.semaphore_wait(barrier, n_z - 1 + n_out + n_out - 1)
@@ -266,11 +268,10 @@
             ) * scale
             for half in range(rpc):
                 j = q * rpc + half
-                chosen = spread(mt_ref[...], s * n_in + j, width) > 0.5
                 for c in range(cpr):
                     where_at = pl.ds(region * j + c, rpr, stride=cpr)
                     acc = res_v[where_at, :] + g[half * rpr : (half + 1) * rpr, c * width : (c + 1) * width]
-                    take = chosen[c * rpr : (c + 1) * rpr]
+                    take = chosen_ref[s * n_in + j, c * rpr : (c + 1) * rpr] > 0.5
                     (resid_ref if s == steps - 1 else res_v)[where_at, :] = jnp.where(take, 0.0, acc)
                     sent[s, j, c * rpr : (c + 1) * rpr] = jnp.where(take, acc, 0.0).astype(BF16)
             waiting += [(s, zz) for zz in range(q * rpc // 2, (q + 1) * rpc // 2)]
@@ -351,7 +352,9 @@
         piece = ag.at[pod, zz, core]
         for d in far_pods:
             send(GATHER_O, piece, piece, fr_sem.at[m], outer=outer(d))
-            if m == n_z - 1:
+
+        if m == n_z - 1:
+            for d in far_pods:
                 send(GATHER_O, piece, piece, g_sem.at[HAND], outer=outer(d), inner=partner)
 
     def hand_over(q, m):
@@ -475,6 +478,7 @@
             pltpu.VMEM((n_z, region, width), BF16),
             pltpu.VMEM((n_z, region, width), BF16),
             pltpu.VMEM((region, width), F32),
+            pltpu.VMEM((steps * n_in, region, width), F32),
             pltpu.VMEM((n_sent, LANES), F32),
             dma((6 + steps,)),
             dma((1,)),

time: 26.1 us -> 25.9 us (level)
  no operation moved by 1% of the time
where the time goes in v5:
time: 25.9 us; the launch traced here: 25.7 us
  Pallas kernels  25.1 us (97%)
  between operations  0.64 us (2%)
    pallas_call x1, Pallas kernels, per_device_fused(): pl.pallas_call(functools.partial(fused_kernel, (n_in, n_out, steps, scale...  23.8 us
    pallas_call x1, Pallas kernels, hand_out(): pl.pallas_call(kernel, out_shape=(jax.ShapeDtypeStruct((rows, pods * widt...  1.24 us

profile of v5, /device:TPU:0, one launch (start us, length us, event | category | flops | bytes accessed | tf_op | source)
XLA Modules:
  0.0 25.7 jit_solution(16906750819034501418)
XLA Ops:
  0.6 23.8 %shard_map.103 = (bf16[4,4,2,64,128]{4,3,2,1,0:T(8,128)(2,1)S(1)}, f32[2048,128]{1,0:T(8,128)S(1)}, f32[256,128]{1,0:T(8,128)S(1)}) custom-call(bf16[2,512,512]{2,1,0:T(8,128)(2,1)} %bitcast.11, bf16[2,512,512]{2,1,0:T(8,128)(2,1)} %bitcast.12, f32[2048,128]{1,0:T(8,128)} %bitcast.13, f32[256,128]{1,0:T(8,128)} %bitcast.14, s32[2,8]{1,0:T(2,128)} %bitcast.17, ...), custom_call_target="tpu_custom_call" | custom-call | tf_op jit(solution)/shard_map/pallas_call | solution.py:449
  24.5 1.2 %shard_map.104 = (bf16[512,512]{1,0:T(8,128)(2,1)}, f32[2048,128]{1,0:T(8,128)}, f32[256,128]{1,0:T(8,128)}) custom-call(bf16[4,512,128]{2,1,0:T(8,128)(2,1)S(1)} %bitcast.10, f32[2048,128]{1,0:T(8,128)S(1)} %get-tuple-element.10.refs_1_, f32[256,128]{1,0:T(8,128)S(1)} %get-tuple-element.11.refs_2_), custom_call_target="tpu_custom_call" | custom-call | tf_op jit(solution)/shard_map/pallas_call | solution.py:406
